TPU v7x, 256 devices: a whole 4x4x8 slice. The times are simulated.
256 devices in a mesh: group: 32 (over z, y_hi, core), mp: 8 (over x, y_lo).
Axes of the slice: x: 4, y: 4 (y_hi: 2, y_lo: 2; y = y_hi * 2 + y_lo), z: 8, core: 2. Of those that a mesh axis runs over, the one named last changes fastest.
Arguments:
- anchor: float32 [16, 2048, 2048], P(None, 'group', 'mp'), may hold values from -6 to 6
- momentum: float32 [16, 2048, 2048], P(None, 'group', 'mp'), may hold values from -3 to 3
- deltas: float32 [32, 2, 2048, 2048], P('group', None, None, 'mp'), may hold values from -3 to 3
- old_path: int32 [32, 2], replicated, may hold values from 0 to 7, as said below
- new_path: int32 [32, 2], replicated, may hold values from 0 to 7, as said below
- tokens: bfloat16 [32, 1024, 2048], P('group', None, 'mp'), may hold values from -40 to 40
- cotangent: bfloat16 [32, 1024, 2048], P('group', None, 'mp'), may hold values from -6 to 6
Outputs:
- new_anchor: float32 [16, 2048, 2048], P(None, 'group', 'mp')
- new_momentum: float32 [16, 2048, 2048], P(None, 'group', 'mp')
- grads: bfloat16 [32, 2, 2048, 2048], P('group', None, None, 'mp')
Inputs may be any that keep to these rules, and one draw needn't show every extreme that they name: `old_path`: for each of the 2 levels, every one of the 8 modules is named by at least one group. `new_path`: for each of the 2 levels, every one of the 8 modules is named by at least one group.
All inputs are finite; a program needn't handle non-finite values.
Results may differ from a plain program's by a relative error of at most 0.014.
Values may be sent and summed in bfloat16 or wider, within the bound.
A program may use at most 128 MiB of HBM per device.

v0:
```python
import math
import jax
import jax.numpy as jnp
from jax import lax
from jax.sharding import Mesh
from jax.sharding import PartitionSpec as P

D = 2048
MODS = 8
MP = ("mp_0", "mp_1")
outer_rate = 0.7
momentum_rate = 0.9
epsilon = 1e-06


def whole_of(x, axes, dim):
    for axis in reversed(axes):
        x = lax.all_gather(x, axis, axis=dim, tiled=True)
    return x


def cut_along(x, dim, length):
    before, after = (x.shape[:dim], x.shape[dim + 1 :])
    return jnp.moveaxis(x.reshape(*before, length, -1, *after), dim, 0)


def summed_on_arrival(x, axis, dim):
    length = lax.axis_size(axis)
    pieces = lax.all_to_all(cut_along(x, dim, length), axis, 0, 0, tiled=True)
    return jnp.sum(pieces.astype(jnp.float32), axis=0)


def silu_slope(values):
    sigmoid_part = jax.nn.sigmoid(values)
    return sigmoid_part * (1.0 + values * (1.0 - sigmoid_part))


def normalize(hidden):
    whole = whole_of(hidden, MP, 1)
    values = whole.astype(jnp.float32)
    scale = lax.rsqrt(jnp.mean(values * values, axis=-1) + epsilon)
    normed = (values * scale[:, None]).astype(jnp.bfloat16)
    return (normed, scale)


def outer_update(received, anchor_rows, momentum_rows, old_columns, new_columns):
    groups_count = received.shape[0]
    levels_count = received.shape[1]
    module_count = anchor_rows.shape[0]
    offsets = jnp.arange(levels_count, dtype=jnp.int32) * MODS
    old_index = (old_columns + offsets[None, :]).reshape(-1)
    selector = (old_index[None, :] == jnp.arange(module_count, dtype=jnp.int32)[:, None]).astype(
        jnp.float32
    )
    sums = jnp.dot(
        selector, received.reshape(groups_count * levels_count, -1), precision=lax.Precision.HIGHEST
    )
    counts = jnp.sum(selector, axis=1)
    outer_grad = (sums / counts[:, None]).reshape(anchor_rows.shape)
    new_momentum = momentum_rate * momentum_rows + outer_grad
    new_anchor = anchor_rows - outer_rate * (outer_grad + momentum_rate * new_momentum)
    new_index = new_columns + offsets[None, :]
    outgoing = jnp.take(new_anchor, new_index, axis=0).astype(jnp.bfloat16)
    return (new_anchor, new_momentum, outgoing)


def shards(anchor, momentum, deltas, old_path, new_path, tokens, cotangent):
    factor = 1.0 / math.sqrt(D)
    first_state = tokens[0]
    upstream = cotangent[0].astype(jnp.float32)
    first_normed, first_scale = normalize(first_state)
    received = lax.all_to_all(
        deltas.astype(jnp.bfloat16), "group", split_axis=2, concat_axis=0, tiled=True
    ).astype(deltas.dtype)
    new_anchor, new_momentum, outgoing = outer_update(
        received, anchor, momentum, old_path, new_path
    )
    loaded = lax.all_to_all(outgoing, "group", split_axis=0, concat_axis=2, tiled=True)
    weight_parts = [loaded[0, 0], loaded[0, 1]]
    first_weight = weight_parts[0]
    second_weight = weight_parts[1]
    first_pre = jnp.dot(first_normed, first_weight, preferred_element_type=jnp.float32) * factor
    second_state = (first_state.astype(jnp.float32) + jax.nn.silu(first_pre)).astype(jnp.bfloat16)
    second_normed, second_scale = normalize(second_state)
    second_pre = jnp.dot(second_normed, second_weight, preferred_element_type=jnp.float32) * factor
    second_slope = (upstream * silu_slope(second_pre)).astype(jnp.bfloat16)
    second_grad = (
        lax.dot_general(
            second_normed,
            second_slope,
            (((0,), (0,)), ((), ())),
            preferred_element_type=jnp.float32,
        )
        * factor
    ).astype(jnp.bfloat16)
    terms = (
        lax.dot_general(
            second_slope,
            second_weight,
            (((1,), (1,)), ((), ())),
            preferred_element_type=jnp.float32,
        )
        * factor
    )
    normed_grad = summed_on_arrival(terms.astype(jnp.bfloat16), MP, 1)
    middle = second_state.astype(jnp.float32)
    inner = lax.psum(jnp.sum(normed_grad * middle, axis=-1), MP)
    state_grad = (
        upstream
        + second_scale[:, None] * normed_grad
        - middle * (second_scale**3 * inner / D)[:, None]
    )
    first_slope = (state_grad * silu_slope(first_pre)).astype(jnp.bfloat16)
    first_grad = (
        lax.dot_general(
            first_normed, first_slope, (((0,), (0,)), ((), ())), preferred_element_type=jnp.float32
        )
        * factor
    ).astype(jnp.bfloat16)
    grads = jnp.stack([first_grad, second_grad])[None]
    return (new_anchor, new_momentum, grads)


def solution(mesh):
    split = Mesh(mesh.devices.reshape(mesh.shape["group"], 4, 2), ("group", "mp_0", "mp_1"))
    placed = (
        P(None, "group", MP),
        P(None, "group", MP),
        P("group", None, None, MP),
        P(),
        P(),
        P("group", None, MP),
        P("group", None, MP),
    )
    return jax.shard_map(
        shards,
        mesh=split,
        in_specs=placed,
        out_specs=(P(None, "group", MP), P(None, "group", MP), P("group", None, None, MP)),
        check_vma=False,
    )
```

profile of v0, /device:TPU:16, one launch (start us, length us, event | category | flops | bytes accessed | tf_op | source)
XLA Modules:
  0.0 331.8 jit_solution(7924139874974365925)
XLA Ops:
  7.2 8.6 %copy.63 = bf16[1,2,2048,256]{3,1,0,2:T(2,128)(2,1)} copy(f32[1,2,2048,256]{3,2,1,0:T(8,128)} %param.9) | data formatting | bytes 6291456 | tf_op args[2]
  15.7 11.7 %all-to-all-start = ((bf16[1,2,2048,256]{3,1,0,2:T(2,128)(2,1)}), bf16[1,2,2048,256]{3,1,0,2:T(2,128)(2,1)S(1)}, u32[]{:S(2)}, u32[]{:S(2)}) async-start(bf16[1,2,2048,256]{3,1,0,2:T(2,128)(2,1)} %copy.63), calls=%async_computation | async-start | bytes 4194304 | tf_op jit(solution)/shard_map/all_to_all | solution.py:72
  27.5 0.7 all-gather.11.cloned.1.call-update
  28.2 36.0 %all-gather.11.cloned.1.call-done = bf16[1,1024,512]{2,1,0:T(8,128)(2,1)} async-done(((bf16[1,1024,256]{2,1,0:T(8,128)(2,1)}), bf16[1,1024,512]{2,1,0:T(8,128)(2,1)}) %all-gather.11.cloned.1.call-update) | async-done | bytes 1048592 | tf_op jit(solution)/shard_map/all_gather | solution.py:18
  65.1 12.5 %all-to-all-done = bf16[1,2,2048,256]{3,1,0,2:T(2,128)(2,1)S(1)} async-done(((bf16[1,2,2048,256]{3,1,0,2:T(2,128)(2,1)}), bf16[1,2,2048,256]{3,1,0,2:T(2,128)(2,1)S(1)}, u32[]{:S(2)}, u32[]{:S(2)}) %all-to-all-start) | async-done | bytes 2097184 | tf_op jit(solution)/shard_map/all_to_all | solution.py:72
  77.6 0.4 copy.45
  78.1 1.3 copy.59
  79.4 0.4 convolution_divide_fusion
  80.1 0.5 copy-done.7
  80.6 0.4 copy-done.8
  81.0 1.3 fusion.34
  82.4 0.8 gather_fusion
  83.1 1.7 select_convert_fusion
  84.9 6.4 %all-to-all-start.1 = ((bf16[32,2,64,256]{3,2,1,0:T(8,128)(2,1)}), bf16[32,2,64,256]{3,2,1,0:T(8,128)(2,1)S(1)}, u32[]{:S(2)}, u32[]{:S(2)}) async-start(bf16[32,2,64,256]{3,2,1,0:T(8,128)(2,1)} %select_convert_fusion), calls=%async_computation.1 | async-start | bytes 4194304 | tf_op jit(solution)/shard_map/all_to_all | solution.py:78
  91.5 28.5 %all-gather.13.cloned.1.call-done = bf16[1,1024,2048]{2,1,0:T(8,128)(2,1)} async-done(((bf16[1,1024,512]{2,1,0:T(8,128)(2,1)}), bf16[1,1024,2048]{2,1,0:T(8,128)(2,1)}) %all-gather.13.cloned.1.call-update) | async-done | bytes 4194320 | tf_op jit(solution)/shard_map/all_gather | solution.py:18
  120.0 3.1 fusion.2
  123.1 18.3 %all-to-all-done.1 = bf16[32,2,64,256]{3,2,1,0:T(8,128)(2,1)S(1)} async-done(((bf16[32,2,64,256]{3,2,1,0:T(8,128)(2,1)}), bf16[32,2,64,256]{3,2,1,0:T(8,128)(2,1)S(1)}, u32[]{:S(2)}, u32[]{:S(2)}) %all-to-all-start.1) | async-done | bytes 2097184 | tf_op jit(solution)/shard_map/all_to_all | solution.py:78
  141.6 2.8 copy-done.1
  144.4 2.8 fusion.35
  147.5 23.5 %all-gather.7.cloned.1.call-done = bf16[1024,512]{0,1:T(8,128)(2,1)} async-done(((bf16[1024,256]{0,1:T(8,128)(2,1)}), bf16[1024,512]{0,1:T(8,128)(2,1)}) %all-gather.7.cloned.1.call-update) | async-done | bytes 1048592 | tf_op jit(solution)/shard_map/all_gather | solution.py:18
  171.2 53.5 %all-gather.9.cloned.1.call-done = bf16[1024,2048]{0,1:T(8,128)(2,1)} async-done(((bf16[1024,512]{0,1:T(8,128)(2,1)}), bf16[1024,2048]{0,1:T(8,128)(2,1)}) %all-gather.9.cloned.1.call-update) | async-done | bytes 4194320 | tf_op jit(solution)/shard_map/all_gather | solution.py:18
  224.6 3.3 fusion
  228.1 1.3 fusion.25
  229.4 1.6 multiply_convert_fusion
  231.1 2.2 copy.64
  233.3 4.7 %all-to-all-start.2 = ((bf16[8,1024,256]{2,1,0:T(8,128)(2,1)}), bf16[8,1024,256]{2,1,0:T(8,128)(2,1)}, u32[]{:S(2)}, u32[]{:S(2)}) async-start(bf16[8,1024,256]{2,1,0:T(8,128)(2,1)} %bitcast.70), calls=%async_computation.2 | async-start | bytes 8388608 | tf_op jit(solution)/shard_map/all_to_all | solution.py:29
  238.0 4.6 %fusion.15 = bf16[1,2048,256]{2,1,0:T(8,128)(2,1)} fusion(bf16[1024,2048]{0,1:T(8,128)(2,1)} %all-gather.9.cloned.1.call-done, f32[1024]{0:T(1024)S(1)} %add_rsqrt_fusion, f32[1024,256]{0,1:T(8,128)S(1)} %copy-done.14, bf16[1,1024,256]{1,2,0:T(8,128)(2,1)S(1)} %copy.46), kind=kOutput, calls=%fused_computation.21 | convolution fusion | flops 1083703296 | bytes 6819840 | tf_op jit(solution)/shard_map/dot_general | solution.py:88
  242.7 55.0 %all-to-all-done.2 = bf16[8,1024,256]{2,1,0:T(8,128)(2,1)} async-done(((bf16[8,1024,256]{2,1,0:T(8,128)(2,1)}), bf16[8,1024,256]{2,1,0:T(8,128)(2,1)}, u32[]{:S(2)}, u32[]{:S(2)}) %all-to-all-start.2) | async-done | bytes 4194336 | tf_op jit(solution)/shard_map/all_to_all | solution.py:29
  297.7 2.9 convert_reduce_fusion
  301.0 18.3 %psum.7 = f32[1024]{0:T(1024)S(1)} all-reduce(f32[1024]{0:T(1024)S(1)} %fusion.28), channel_id=1, replica_groups=mesh['group'=32,'mp_0'=4,'mp_1'=2] {'mp_0','mp_1'}, use_global_device_ids=true, to_apply=%region_5.6 | all-reduce | flops 1024 | bytes 8192 | tf_op jit(solution)/shard_map/psum | solution.py:107
  319.3 4.5 %fusion.18 = bf16[1,2048,256]{2,1,0:T(8,128)(2,1)S(1)} fusion(bf16[1,1024,2048]{2,1,0:T(8,128)(2,1)} %all-gather.13.cloned.1.call-done, f32[1024]{0:T(1024)S(1)} %add_rsqrt_fusion.1, bf16[1024,256]{0,1:T(8,128)(2,1)S(1)} %copy-done.3, f32[1024,256]{0,1:T(8,128)} %get-tuple-element.8, f32[1024,256]{0,1:T(8,128)S(1)} %copy.54, ...), kind=kOutput, calls=%fused_computation.22 | convolution fusion | flops 1085014016 | bytes 8400896 | tf_op jit(solution)/shard_map/dot_general | solution.py:115
  323.8 1.5 maximum_bitcast_fusion
  (53 shorter events, 2.8 us)
Async XLA Ops:
  15.7 48.6 %copy-start.11 = (s32[32,2]{0,1:T(2,128)S(1)}, s32[32,2]{0,1:T(2,128)}, u32[]{:S(2)}) copy-start(s32[32,2]{0,1:T(2,128)} %param.11) | copy-start | bytes 772
  15.7 48.8 %copy-start.12 = (s32[32,2]{0,1:T(2,128)S(1)}, s32[32,2]{0,1:T(2,128)}, u32[]{:S(2)}) copy-start(s32[32,2]{0,1:T(2,128)} %param.10) | copy-start | bytes 772
  15.7 61.9 %all-to-all-start = ((bf16[1,2,2048,256]{3,1,0,2:T(2,128)(2,1)}), bf16[1,2,2048,256]{3,1,0,2:T(2,128)(2,1)S(1)}, u32[]{:S(2)}, u32[]{:S(2)}) async-start(bf16[1,2,2048,256]{3,1,0,2:T(2,128)(2,1)} %copy.63), calls=%async_computation | async-start | bytes 4194304 | tf_op jit(solution)/shard_map/all_to_all | solution.py:72
  27.5 36.8 %all-gather.11.cloned.1.call-start = ((), (), s32[]{:S(2)}) async-start(), calls=%async_computation.5 | async-start | bytes 1572864 | tf_op jit(solution)/shard_map/all_gather | solution.py:18
  28.2 91.8 %all-gather.13.cloned.1.call-start = ((), (), s32[]{:S(2)}) async-start(), calls=%async_computation.6 | async-start | bytes 5242880 | tf_op jit(solution)/shard_map/all_gather | solution.py:18
  79.3 1.3 copy-start.7
  79.4 1.7 copy-start.8
  82.4 2.5 copy-start
  84.9 6.4 %copy-start.6 = (bf16[1,1024,256]{2,1,0:T(8,128)(2,1)S(1)}, bf16[1,1024,256]{2,1,0:T(8,128)(2,1)}, u32[]{:S(2)}) copy-start(bf16[1,1024,256]{2,1,0:T(8,128)(2,1)} %param.12) | copy-start | bytes 1572868
  84.9 56.6 %all-to-all-start.1 = ((bf16[32,2,64,256]{3,2,1,0:T(8,128)(2,1)}), bf16[32,2,64,256]{3,2,1,0:T(8,128)(2,1)S(1)}, u32[]{:S(2)}, u32[]{:S(2)}) async-start(bf16[32,2,64,256]{3,2,1,0:T(8,128)(2,1)} %select_convert_fusion), calls=%async_computation.1 | async-start | bytes 4194304 | tf_op jit(solution)/shard_map/all_to_all | solution.py:78
  91.3 79.7 %all-gather.7.cloned.1.call-start = ((), (), s32[]{:S(2)}) async-start(), calls=%async_computation.3 | async-start | bytes 1572864 | tf_op jit(solution)/shard_map/all_gather | solution.py:18
  141.4 2.9 copy-start.1
  141.6 5.6 %copy-start.4 = (bf16[1,2,32,64,256]{4,3,2,1,0:T(8,128)(2,1)}, bf16[1,2,32,64,256]{4,3,2,1,0:T(8,128)(2,1)S(1)}, u32[]{:S(2)}) copy-start(bf16[1,2,32,64,256]{4,3,2,1,0:T(8,128)(2,1)S(1)} %copy.50) | copy-start | bytes 6291460
  144.4 26.6 %copy-start.10 = (bf16[1,1024,256]{2,1,0:T(8,128)(2,1)S(1)}, bf16[1,1024,256]{2,1,0:T(8,128)(2,1)}, u32[]{:S(2)}) copy-start(bf16[1,1024,256]{2,1,0:T(8,128)(2,1)} %param.13) | copy-start | bytes 1572868
  147.2 80.7 %copy-start.5 = (bf16[1,2,32,64,256]{4,3,2,1,0:T(8,128)(2,1)S(1)}, bf16[1,2,32,64,256]{4,3,2,1,0:T(8,128)(2,1)}, u32[]{:S(2)}) copy-start(bf16[1,2,32,64,256]{4,3,2,1,0:T(8,128)(2,1)} %copy-done.4) | copy-start | bytes 6291460
  147.2 77.4 %all-gather.9.cloned.1.call-start = ((), (), s32[]{:S(2)}) async-start(), calls=%async_computation.4 | async-start | bytes 5242880 | tf_op jit(solution)/shard_map/all_gather | solution.py:18
  224.6 3.4 %copy-start.2 = (bf16[1024,2048]{0,1:T(8,128)(2,1)S(1)}, bf16[1024,2048]{0,1:T(8,128)(2,1)}, u32[]{:S(2)}) copy-start(bf16[1024,2048]{0,1:T(8,128)(2,1)} %all-gather.9.cloned.1.call-done) | copy-start | bytes 12582916
  229.4 1.7 copy-start.13
  233.3 4.7 %copy-start.14 = (f32[1024,256]{0,1:T(8,128)S(1)}, f32[1024,256]{0,1:T(8,128)}, u32[]{:S(2)}) copy-start(f32[1024,256]{0,1:T(8,128)} %copy-done.13) | copy-start | bytes 3145732
  233.3 64.4 %all-to-all-start.2 = ((bf16[8,1024,256]{2,1,0:T(8,128)(2,1)}), bf16[8,1024,256]{2,1,0:T(8,128)(2,1)}, u32[]{:S(2)}, u32[]{:S(2)}) async-start(bf16[8,1024,256]{2,1,0:T(8,128)(2,1)} %bitcast.70), calls=%async_computation.2 | async-start | bytes 8388608 | tf_op jit(solution)/shard_map/all_to_all | solution.py:29
  242.7 58.2 %copy-start.3 = (bf16[1024,256]{0,1:T(8,128)(2,1)S(1)}, bf16[1024,256]{0,1:T(8,128)(2,1)}, u32[]{:S(2)}) copy-start(bf16[1024,256]{0,1:T(8,128)(2,1)} %get-tuple-element.7) | copy-start | bytes 1572868
  319.3 4.5 %copy-start.9 = (bf16[1,2048,256]{2,1,0:T(8,128)(2,1)S(1)}, bf16[1,2048,256]{2,1,0:T(8,128)(2,1)}, u32[]{:S(2)}) copy-start(bf16[1,2048,256]{2,1,0:T(8,128)(2,1)} %fusion.15) | copy-start | bytes 3145732
Sparse Core Ops, SparseCore 0:
  30.1 34.1 all-gather.10
  66.1 53.8 all-gather.12
  147.4 23.5 all-gather.6
  172.6 52.0 all-gather.8
where the time goes:
time: 332 us
  waiting for transfers between devices  228 us (69%)
  starting transfers between devices  23.2 us (7%)
  local copies, waits for them, and re-layouts  18.9 us (6%)
  blocking collectives  18.3 us (6%)
  matrix products  15.3 us (5%)
  other arithmetic  14.2 us (4%)
  between operations  14 us (4%)
    all_gather x4, waiting for transfers between devices, whole_of(): x = lax.all_gather(x, axis, axis=dim, tiled=True)  141 us
    all_to_all x1, waiting for transfers between devices, summed_on_arrival(): pieces = lax.all_to_all(cut_along(x, dim, length), axis, 0, 0, tiled=True)  55 us
    all_to_all x1, waiting for transfers between devices, shards(): lax.all_to_all(outgoing, 'group', split_axis=0, concat_axis=2, tiled=True)  18.3 us
    psum x1, blocking collectives, shards(): inner = lax.psum(jnp.sum(normed_grad * middle, axis=-1), MP)  18.3 us
    unnamed x35, local copies, waits for them, and re-layouts  14.5 us
    all_to_all x1, waiting for transfers between devices, shards(): lax.all_to_all(deltas.astype(jnp.bfloat16), 'group', split_axis=2, concat...  12.5 us
    all_to_all x1, starting transfers between devices, shards(): lax.all_to_all(deltas.astype(jnp.bfloat16), 'group', split_axis=2, concat...  11.7 us
  transfers between devices with their start and end apart: 7, of which 7 were waited for; matrix products, arithmetic and copies ran while one was open for 5% of the time, Pallas kernels for 0%

commit v1 on v0

--- a/solution.py
+++ b/solution.py
@@ -75,7 +75,15 @@
     new_anchor, new_momentum, outgoing = outer_update(
         received, anchor, momentum, old_path, new_path
     )
-    loaded = lax.all_to_all(outgoing, "group", split_axis=0, concat_axis=2, tiled=True)
+    loaded = jnp.concatenate(
+        lax.all_to_all(
+            jnp.stack(jnp.split(outgoing, lax.psum(1, axis_name="group"), axis=0)),
+            axis_name="group",
+            split_axis=0,
+            concat_axis=0,
+        ),
+        axis=2,
+    )
     weight_parts = [loaded[0, 0], loaded[0, 1]]
     first_weight = weight_parts[0]
     second_weight = weight_parts[1]

time: 332 us -> 353 us (1.063)
  local copies, waits for them, and re-layouts: 18.9 us -> 40.5 us
    unnamed x35 -> x66, local copies, waits for them, and re-layouts: 14.5 us -> 35.5 us
    all_gather x4, waiting for transfers between devices: 141 us -> 121 us  [whole_of(): x = lax.all_gather(x, axis, axis=dim, tiled=True)]
    all_to_all x1, waiting for transfers between devices: 18.3 us -> 37.9 us  [shards(): lax.all_to_all(jnp.stack(jnp.split(outgoing, lax.psum(1, axis_name='group...]
  transfers between devices with their start and end apart: 7 -> 7, of which waited for: 7 -> 7; matrix products, arithmetic and copies ran while one was open for 5% -> 10% of each run, Pallas kernels for 0% -> 0%
where the time goes in v1:
time: 353 us; the launch traced here: 352 us
  waiting for transfers between devices  228 us (65%)
  local copies, waits for them, and re-layouts  40.5 us (11%)
  starting transfers between devices  23.1 us (7%)
  blocking collectives  18.3 us (5%)
  matrix products  15.3 us (4%)
  between operations  14 us (4%)
  other arithmetic  12.9 us (4%)
    all_gather x4, waiting for transfers between devices, whole_of(): x = lax.all_gather(x, axis, axis=dim, tiled=True)  121 us
    all_to_all x1, waiting for transfers between devices, summed_on_arrival(): pieces = lax.all_to_all(cut_along(x, dim, length), axis, 0, 0, tiled=True)  55 us
    all_to_all x1, waiting for transfers between devices, shards(): lax.all_to_all(jnp.stack(jnp.split(outgoing, lax.psum(1, axis_name='group...  37.9 us
    unnamed x66, local copies, waits for them, and re-layouts  35.5 us
    psum x1, blocking collectives, shards(): inner = lax.psum(jnp.sum(normed_grad * middle, axis=-1), MP)  18.3 us
    all_to_all x1, waiting for transfers between devices, shards(): lax.all_to_all(deltas.astype(jnp.bfloat16), 'group', split_axis=2, concat...  13.3 us
    all_to_all x1, starting transfers between devices, shards(): lax.all_to_all(deltas.astype(jnp.bfloat16), 'group', split_axis=2, concat...  11.7 us
  transfers between devices with their start and end apart: 7, of which 7 were waited for; matrix products, arithmetic and copies ran while one was open for 10% of the time, Pallas kernels for 0%

profile of v1, /device:TPU:16, one launch (start us, length us, event | category | flops | bytes accessed | tf_op | source)
XLA Modules:
  0.0 352.1 jit_solution(1747499497317735349)
XLA Ops:
  7.2 8.6 %copy.87 = bf16[1,2,2048,256]{3,1,0,2:T(2,128)(2,1)} copy(f32[1,2,2048,256]{3,2,1,0:T(8,128)} %param.9) | data formatting | bytes 6291456 | tf_op args[2]
  15.7 11.7 %all-to-all-start = ((bf16[1,2,2048,256]{3,1,0,2:T(2,128)(2,1)}), bf16[1,2,2048,256]{3,1,0,2:T(2,128)(2,1)S(1)}, u32[]{:S(2)}, u32[]{:S(2)}) async-start(bf16[1,2,2048,256]{3,1,0,2:T(2,128)(2,1)} %copy.87), calls=%async_computation | async-start | bytes 4194304 | tf_op jit(solution)/shard_map/all_to_all | solution.py:72
  27.5 0.7 all-gather.11.cloned.1.call-update
  29.1 35.2 %all-gather.11.cloned.1.call-done = bf16[1,1024,512]{2,1,0:T(8,128)(2,1)} async-done(((bf16[1,1024,256]{2,1,0:T(8,128)(2,1)}), bf16[1,1024,512]{2,1,0:T(8,128)(2,1)}) %all-gather.11.cloned.1.call-update) | async-done | bytes 1048592 | tf_op jit(solution)/shard_map/all_gather | solution.py:18
  64.3 13.3 %all-to-all-done = bf16[1,2,2048,256]{3,1,0,2:T(2,128)(2,1)S(1)} async-done(((bf16[1,2,2048,256]{3,1,0,2:T(2,128)(2,1)}), bf16[1,2,2048,256]{3,1,0,2:T(2,128)(2,1)S(1)}, u32[]{:S(2)}, u32[]{:S(2)}) %all-to-all-start) | async-done | bytes 2097184 | tf_op jit(solution)/shard_map/all_to_all | solution.py:72
  78.1 1.3 copy.83
  80.1 1.0 copy-done.7
  81.5 1.3 fusion.34
  82.8 0.8 gather_fusion
  84.2 0.6 fusion.78
  90.5 0.6 fusion.68
  91.8 0.6 fusion.66
  104.5 6.3 %all-to-all-start.1 = ((bf16[32,1,2,64,256]{4,3,2,1,0:T(8,128)(2,1)}), bf16[32,1,2,64,256]{4,3,2,1,0:T(8,128)(2,1)S(1)}, u32[]{:S(2)}, u32[]{:S(2)}) async-start(bf16[32,1,2,64,256]{4,3,2,1,0:T(8,128)(2,1)} %fusion.47), calls=%async_computation.1 | async-start | bytes 4194304 | tf_op jit(solution)/shard_map/all_to_all | solution.py:79
  111.1 8.9 %all-gather.13.cloned.1.call-done = bf16[1,1024,2048]{2,1,0:T(8,128)(2,1)} async-done(((bf16[1,1024,512]{2,1,0:T(8,128)(2,1)}), bf16[1,1024,2048]{2,1,0:T(8,128)(2,1)}) %all-gather.13.cloned.1.call-update) | async-done | bytes 4194320 | tf_op jit(solution)/shard_map/all_gather | solution.py:18
  120.0 3.1 fusion.2
  123.1 37.9 %all-to-all-done.1 = bf16[32,1,2,64,256]{4,3,2,1,0:T(8,128)(2,1)S(1)} async-done(((bf16[32,1,2,64,256]{4,3,2,1,0:T(8,128)(2,1)}), bf16[32,1,2,64,256]{4,3,2,1,0:T(8,128)(2,1)S(1)}, u32[]{:S(2)}, u32[]{:S(2)}) %all-to-all-start.1) | async-done | bytes 2097184 | tf_op jit(solution)/shard_map/all_to_all | solution.py:79
  161.1 2.8 copy-done.1
  163.9 2.8 fusion.35
  167.0 23.5 %all-gather.7.cloned.1.call-done = bf16[1024,512]{0,1:T(8,128)(2,1)} async-done(((bf16[1024,256]{0,1:T(8,128)(2,1)}), bf16[1024,512]{0,1:T(8,128)(2,1)}) %all-gather.7.cloned.1.call-update) | async-done | bytes 1048592 | tf_op jit(solution)/shard_map/all_gather | solution.py:18
  190.7 53.5 %all-gather.9.cloned.1.call-done = bf16[1024,2048]{0,1:T(8,128)(2,1)} async-done(((bf16[1024,512]{0,1:T(8,128)(2,1)}), bf16[1024,2048]{0,1:T(8,128)(2,1)}) %all-gather.9.cloned.1.call-update) | async-done | bytes 4194320 | tf_op jit(solution)/shard_map/all_gather | solution.py:18
  244.2 3.3 fusion
  247.7 1.3 fusion.25
  249.0 1.6 multiply_convert_fusion
  250.7 2.2 copy.88
  252.9 4.7 %all-to-all-start.2 = ((bf16[8,1024,256]{2,1,0:T(8,128)(2,1)}), bf16[8,1024,256]{2,1,0:T(8,128)(2,1)}, u32[]{:S(2)}, u32[]{:S(2)}) async-start(bf16[8,1024,256]{2,1,0:T(8,128)(2,1)} %bitcast.197), calls=%async_computation.2 | async-start | bytes 8388608 | tf_op jit(solution)/shard_map/all_to_all | solution.py:29
  257.6 4.6 %fusion.15 = bf16[1,2048,256]{2,1,0:T(8,128)(2,1)} fusion(bf16[1024,2048]{0,1:T(8,128)(2,1)} %all-gather.9.cloned.1.call-done, f32[1024]{0:T(1024)S(1)} %add_rsqrt_fusion, f32[1024,256]{0,1:T(8,128)S(1)} %copy-done.14, bf16[1,1024,256]{1,2,0:T(8,128)(2,1)S(1)} %copy.70), kind=kOutput, calls=%fused_computation.21 | convolution fusion | flops 1083703296 | bytes 6819840 | tf_op jit(solution)/shard_map/dot_general | solution.py:96
  262.2 55.0 %all-to-all-done.2 = bf16[8,1024,256]{2,1,0:T(8,128)(2,1)} async-done(((bf16[8,1024,256]{2,1,0:T(8,128)(2,1)}), bf16[8,1024,256]{2,1,0:T(8,128)(2,1)}, u32[]{:S(2)}, u32[]{:S(2)}) %all-to-all-start.2) | async-done | bytes 4194336 | tf_op jit(solution)/shard_map/all_to_all | solution.py:29
  317.2 2.9 convert_reduce_fusion
  320.5 0.7 copy-done.3
  321.3 18.3 %psum.7 = f32[1024]{0:T(1024)S(1)} all-reduce(f32[1024]{0:T(1024)S(1)} %fusion.28), channel_id=1, replica_groups=mesh['group'=32,'mp_0'=4,'mp_1'=2] {'mp_0','mp_1'}, use_global_device_ids=true, to_apply=%region_5.6 | all-reduce | flops 1024 | bytes 8192 | tf_op jit(solution)/shard_map/psum | solution.py:115
  339.6 4.5 %fusion.18 = bf16[1,2048,256]{2,1,0:T(8,128)(2,1)S(1)} fusion(bf16[1,1024,2048]{2,1,0:T(8,128)(2,1)} %all-gather.13.cloned.1.call-done, f32[1024]{0:T(1024)S(1)} %add_rsqrt_fusion.1, bf16[1024,256]{0,1:T(8,128)(2,1)S(1)} %copy-done.3, f32[1024,256]{0,1:T(8,128)} %get-tuple-element.8, f32[1024,256]{0,1:T(8,128)S(1)} %copy.78, ...), kind=kOutput, calls=%fused_computation.22 | convolution fusion | flops 1085014016 | bytes 8400896 | tf_op jit(solution)/shard_map/dot_general | solution.py:123
  344.1 1.5 maximum_bitcast_fusion
  (85 shorter events, 23.0 us)
Async XLA Ops:
  15.7 12.5 %copy-start.11 = (s32[32,2]{0,1:T(2,128)S(1)}, s32[32,2]{0,1:T(2,128)}, u32[]{:S(2)}) copy-start(s32[32,2]{0,1:T(2,128)} %param.11) | copy-start | bytes 772
  15.7 12.7 %copy-start.12 = (s32[32,2]{0,1:T(2,128)S(1)}, s32[32,2]{0,1:T(2,128)}, u32[]{:S(2)}) copy-start(s32[32,2]{0,1:T(2,128)} %param.10) | copy-start | bytes 772
  15.7 61.9 %all-to-all-start = ((bf16[1,2,2048,256]{3,1,0,2:T(2,128)(2,1)}), bf16[1,2,2048,256]{3,1,0,2:T(2,128)(2,1)S(1)}, u32[]{:S(2)}, u32[]{:S(2)}) async-start(bf16[1,2,2048,256]{3,1,0,2:T(2,128)(2,1)} %copy.87), calls=%async_computation | async-start | bytes 4194304 | tf_op jit(solution)/shard_map/all_to_all | solution.py:72
  27.5 36.8 %all-gather.11.cloned.1.call-start = ((), (), s32[]{:S(2)}) async-start(), calls=%async_computation.5 | async-start | bytes 1572864 | tf_op jit(solution)/shard_map/all_gather | solution.py:18
  28.2 91.8 %all-gather.13.cloned.1.call-start = ((), (), s32[]{:S(2)}) async-start(), calls=%async_computation.6 | async-start | bytes 5242880 | tf_op jit(solution)/shard_map/all_gather | solution.py:18
  79.7 1.3 copy-start.7
  79.8 1.7 copy-start.8
  82.8 1.0 copy-start
  104.5 6.4 %copy-start.6 = (bf16[1,1024,256]{2,1,0:T(8,128)(2,1)S(1)}, bf16[1,1024,256]{2,1,0:T(8,128)(2,1)}, u32[]{:S(2)}) copy-start(bf16[1,1024,256]{2,1,0:T(8,128)(2,1)} %param.12) | copy-start | bytes 1572868
  104.5 56.5 %all-to-all-start.1 = ((bf16[32,1,2,64,256]{4,3,2,1,0:T(8,128)(2,1)}), bf16[32,1,2,64,256]{4,3,2,1,0:T(8,128)(2,1)S(1)}, u32[]{:S(2)}, u32[]{:S(2)}) async-start(bf16[32,1,2,64,256]{4,3,2,1,0:T(8,128)(2,1)} %fusion.47), calls=%async_computation.1 | async-start | bytes 4194304 | tf_op jit(solution)/shard_map/all_to_all | solution.py:79
  110.8 79.7 %all-gather.7.cloned.1.call-start = ((), (), s32[]{:S(2)}) async-start(), calls=%async_computation.3 | async-start | bytes 1572864 | tf_op jit(solution)/shard_map/all_gather | solution.py:18
  161.0 2.9 copy-start.1
  161.1 5.6 %copy-start.4 = (bf16[32,1,2,64,256]{4,3,0,2,1:T(8,128)(2,1)}, bf16[32,1,2,64,256]{4,3,0,2,1:T(8,128)(2,1)S(1)}, u32[]{:S(2)}) copy-start(bf16[32,1,2,64,256]{4,3,0,2,1:T(8,128)(2,1)S(1)} %copy.74) | copy-start | bytes 6291460
  163.9 26.6 %copy-start.10 = (bf16[1,1024,256]{2,1,0:T(8,128)(2,1)S(1)}, bf16[1,1024,256]{2,1,0:T(8,128)(2,1)}, u32[]{:S(2)}) copy-start(bf16[1,1024,256]{2,1,0:T(8,128)(2,1)} %param.13) | copy-start | bytes 1572868
  166.8 77.4 %all-gather.9.cloned.1.call-start = ((), (), s32[]{:S(2)}) async-start(), calls=%async_computation.4 | async-start | bytes 5242880 | tf_op jit(solution)/shard_map/all_gather | solution.py:18
  190.5 57.0 %copy-start.5 = (bf16[32,1,2,64,256]{4,3,0,2,1:T(8,128)(2,1)S(1)}, bf16[32,1,2,64,256]{4,3,0,2,1:T(8,128)(2,1)}, u32[]{:S(2)}) copy-start(bf16[32,1,2,64,256]{4,3,0,2,1:T(8,128)(2,1)} %copy-done.4) | copy-start | bytes 6291460
  244.2 3.4 copy-start.2
  249.0 1.7 copy-start.13
  252.9 4.7 %copy-start.14 = (f32[1024,256]{0,1:T(8,128)S(1)}, f32[1024,256]{0,1:T(8,128)}, u32[]{:S(2)}) copy-start(f32[1024,256]{0,1:T(8,128)} %copy-done.13) | copy-start | bytes 3145732
  252.9 64.4 %all-to-all-start.2 = ((bf16[8,1024,256]{2,1,0:T(8,128)(2,1)}), bf16[8,1024,256]{2,1,0:T(8,128)(2,1)}, u32[]{:S(2)}, u32[]{:S(2)}) async-start(bf16[8,1024,256]{2,1,0:T(8,128)(2,1)} %bitcast.197), calls=%async_computation.2 | async-start | bytes 8388608 | tf_op jit(solution)/shard_map/all_to_all | solution.py:29
  320.1 1.0 copy-start.3
  339.6 4.5 %copy-start.9 = (bf16[1,2048,256]{2,1,0:T(8,128)(2,1)S(1)}, bf16[1,2048,256]{2,1,0:T(8,128)(2,1)}, u32[]{:S(2)}) copy-start(bf16[1,2048,256]{2,1,0:T(8,128)(2,1)} %fusion.15) | copy-start | bytes 3145732
Sparse Core Ops, SparseCore 0:
  30.1 34.1 all-gather.10
  66.1 53.8 all-gather.12
  166.9 23.5 all-gather.6
  192.2 52.0 all-gather.8
